TPU v7x, 32 devices: a whole 2x2x4 slice. The times are simulated.
32 devices in a mesh: loc: 32 (over z, y, x, core).
Axes of the slice: x: 2, y: 2, z: 4, core: 2. Of those that a mesh axis runs over, the one named last changes fastest.
Arguments:
- hazard_bins: int32 [256, 8192], P(None, 'loc'), may hold values from 0 to 63
- curve_index: int32 [8192], P('loc'), may hold values from 0 to 255
- damage_table: float32 [256, 64], replicated, may hold values from 0.02 to 0.9
- insured_value: float32 [8192], P('loc'), may hold values from 0.5 to 5
- deductible: float32 [8192], P('loc'), may hold values from 0.05 to 0.5
- loss_limit: float32 [8192], P('loc'), may hold values from 0.5 to 3
- uncertainty: float32 [128, 8192], P(None, 'loc'), may hold values from 0.5 to 2
- year_ids: int32 [256], replicated, may hold values from 0 to 63
Outputs:
- event_loss: float32 [256, 128], P('loc')
- year_loss: float32 [64, 128], replicated
All inputs are finite; a program needn't handle non-finite values.
Results may differ from a plain program's by a relative error of at most 0.00005.
Values sent between devices are 32-bit elements; how exact they have to be, the bound alone decides.
A program may use at most 64 MiB of HBM per device.

v0:
```python
import math
import jax
import jax.numpy as jnp
from jax import lax
from jax.sharding import PartitionSpec as P

YEARS = 64


def shards(
    hazard_bins,
    curve_index,
    damage_table,
    insured_value,
    deductible,
    loss_limit,
    uncertainty,
    year_ids,
):
    curve_count = damage_table.shape[0]
    bin_count = damage_table.shape[1]
    selector = (curve_index[None, :] == jnp.arange(curve_count, dtype=jnp.int32)[:, None]).astype(
        jnp.float32
    )
    curve_rows = jnp.dot(
        damage_table.T,
        selector,
        precision=lax.Precision.HIGHEST,
        preferred_element_type=jnp.float32,
    )
    bin_ids = jnp.arange(bin_count, dtype=jnp.int32)[None, :, None]
    shard_width = insured_value.shape[0]
    locations = shard_width * lax.axis_size("loc")
    event_total = hazard_bins.shape[0]
    own_rows = event_total // lax.axis_size("loc")
    year_range = jnp.arange(YEARS, dtype=jnp.int32)
    target_rows = max(16, 32768 // shard_width)
    target_rows = 1 << target_rows.bit_length() - 1

    def block_terms(hazard_block):
        ratios = jnp.sum(
            jnp.where(hazard_block[:, None, :] == bin_ids, curve_rows[None, :, :], 0.0), axis=1
        )
        damage = jnp.minimum(ratios[:, None, :] * uncertainty[None, :, :], 1.0)
        losses = jnp.minimum(jnp.maximum(insured_value * damage - deductible, 0.0), loss_limit)
        return jnp.sum(losses, axis=2)

    block_rows = math.gcd(event_total, target_rows)
    grouped = hazard_bins.reshape(event_total // block_rows, block_rows, hazard_bins.shape[1])
    summed = lax.psum(
        lax.map(block_terms, grouped).reshape(event_total, uncertainty.shape[0]), "loc"
    )
    all_events = summed * (1.0 / locations)
    membership = (year_ids[:, None] == year_range[None, :]).astype(jnp.float32)
    year_loss = jnp.dot(
        membership.T,
        all_events,
        precision=lax.Precision.HIGHEST,
        preferred_element_type=jnp.float32,
    ) * (YEARS / event_total)
    event_loss = lax.dynamic_slice_in_dim(all_events, lax.axis_index("loc") * own_rows, own_rows, 0)
    return (event_loss, year_loss)


def solution(mesh):
    return jax.shard_map(
        shards,
        mesh=mesh,
        in_specs=(P(None, "loc"), P("loc"), P(), P("loc"), P("loc"), P("loc"), P(None, "loc"), P()),
        out_specs=(P("loc", None), P()),
        check_vma=False,
    )
```

profile of v0, /device:TPU:0, one launch (start us, length us, event | category | flops | bytes accessed | tf_op | source)
XLA Modules:
  0.0 161.2 jit_solution(17336315742773112577)
XLA Ops:
  7.2 0.0 copy-start
  7.2 0.0 all-reduce.2.cloned.1.call-start
  7.2 0.8 copy-done
  8.0 0.9 convolution_bitcast_fusion
  8.9 14.9 %while.11 = (s32[]{:T(128)}, f32[2,128,128]{2,1,0:T(8,128)S(1)}, f32[256]{0:T(256)}, s32[2,128,256]{2,1,0:T(8,128)}, f32[64,256]{1,0:T(8,128)S(1)}, /*index=5*/f...) while((s32[]{:T(128)}, f32[2,128,128]{2,1,0:T(8,128)S(1)}, f32[256]{0:T(256)}, ...), condition=%wide.region_3.4_spmd.clone, body=%wide.region_0.3_spmd.clone.sunk | while | flops 35602432 | bytes 1588437 | solution.py:51
  8.9 0.0 copy-start.1
  8.9 0.0 copy-start.4
  9.0 0.0 copy-start.5
  9.0 0.0 copy-start.6
  9.0 1.0 dynamic-slice_bitcast_fusion.2
  10.0 2.4 %select_reduce_fusion.2 = f32[128,256]{1,0:T(8,128)S(1)} fusion(f32[64,256]{1,0:T(8,128)S(1)} %get-tuple-element.155, s32[128,256]{1,0:T(8,128)S(1)} %dynamic-slice_bitcast_fusion.2), kind=kLoop, calls=%fused_computation.3.clone.1 | loop fusion | flops 6258688 | bytes 327680 | tf_op jit(solution)/shard_map/while/body/eval_jaxpr/reduce_sum | solution.py:41
  12.4 0.0 copy-done.1
  12.4 0.0 copy-done.4
  12.4 0.0 copy-done.5
  12.4 0.0 copy-done.6
  12.4 3.9 %minimum_reduce_fusion.2 = f32[128,128]{1,0:T(8,128)S(1)} fusion(f32[256]{0:T(256)S(1)} %copy-done.6, f32[256]{0:T(256)S(1)} %copy-done.5, f32[128,256]{1,0:T(8,128)S(1)} %copy-done.1, f32[128,256]{1,0:T(8,128)S(1)} %select_reduce_fusion.2, f32[256]{0:T(256)S(1)} %copy-done.4), kind=kLoop, calls=%fused_computation.1.clone.1 | loop fusion | flops 29343744 | bytes 330752 | tf_op jit(solution)/shard_map/while/body/eval_jaxpr/reduce_sum | solution.py:46
  16.4 0.0 copy-start.1
  16.4 0.0 copy-start.4
  16.4 0.0 copy-start.5
  16.4 0.0 copy-start.6
  16.4 1.0 dynamic-slice_bitcast_fusion.2
  17.4 2.4 %select_reduce_fusion.2 = f32[128,256]{1,0:T(8,128)S(1)} fusion(f32[64,256]{1,0:T(8,128)S(1)} %get-tuple-element.155, s32[128,256]{1,0:T(8,128)S(1)} %dynamic-slice_bitcast_fusion.2), kind=kLoop, calls=%fused_computation.3.clone.1 | loop fusion | flops 6258688 | bytes 327680 | tf_op jit(solution)/shard_map/while/body/eval_jaxpr/reduce_sum | solution.py:41
  19.8 0.0 copy-done.1
  19.8 0.0 copy-done.4
  19.8 0.0 copy-done.5
  19.8 0.0 copy-done.6
  19.8 3.9 %minimum_reduce_fusion.2 = f32[128,128]{1,0:T(8,128)S(1)} fusion(f32[256]{0:T(256)S(1)} %copy-done.6, f32[256]{0:T(256)S(1)} %copy-done.5, f32[128,256]{1,0:T(8,128)S(1)} %copy-done.1, f32[128,256]{1,0:T(8,128)S(1)} %select_reduce_fusion.2, f32[256]{0:T(256)S(1)} %copy-done.4), kind=kLoop, calls=%fused_computation.1.clone.1 | loop fusion | flops 29343744 | bytes 330752 | tf_op jit(solution)/shard_map/while/body/eval_jaxpr/reduce_sum | solution.py:46
  23.8 0.0 copy-start.3
  23.8 0.0 copy-start.7
  23.8 0.6 copy-done.3
  24.4 0.0 all-reduce.2.cloned.1.call-update
  24.4 127.3 %all-reduce.2.cloned.1.call-done = f32[256,128]{1,0:T(8,128)} async-done(((f32[256,128]{1,0:T(8,128)}), f32[256,128]{1,0:T(8,128)}) %all-reduce.2.cloned.1.call-update) | async-done | bytes 131088 | tf_op jit(solution)/shard_map/psum | solution.py:50
  151.8 0.0 copy-start.2
  151.8 1.0 broadcast_multiply_fusion
  152.8 0.6 constant_dynamic-slice_fusion
  153.4 0.0 copy-done.7
  153.4 0.0 copy-done.2
  153.4 1.0 convolution_multiply_fusion
  (3 shorter events, 0.0 us)
Async XLA Ops:
  7.2 0.8 copy-start
  7.2 144.6 %all-reduce.2.cloned.1.call-start = ((), (), s32[]{:S(2)}) async-start(), calls=%async_computation | async-start | bytes 262144 | tf_op jit(solution)/shard_map/psum | solution.py:50
  8.9 3.4 %copy-start.1 = (f32[128,256]{1,0:T(8,128)S(1)}, f32[128,256]{1,0:T(8,128)}, u32[]{:S(2)}) copy-start(f32[128,256]{1,0:T(8,128)} %get-tuple-element.156) | copy-start | bytes 393220 | tf_op jit(solution)/shard_map/while
  8.9 3.4 %copy-start.4 = (f32[256]{0:T(256)S(1)}, f32[256]{0:T(256)}, u32[]{:S(2)}) copy-start(f32[256]{0:T(256)} %get-tuple-element.153) | copy-start | bytes 3076 | tf_op jit(solution)/shard_map/while
  9.0 3.4 %copy-start.5 = (f32[256]{0:T(256)S(1)}, f32[256]{0:T(256)}, u32[]{:S(2)}) copy-start(f32[256]{0:T(256)} %get-tuple-element.157) | copy-start | bytes 3076 | tf_op jit(solution)/shard_map/while
  9.0 3.4 %copy-start.6 = (f32[256]{0:T(256)S(1)}, f32[256]{0:T(256)}, u32[]{:S(2)}) copy-start(f32[256]{0:T(256)} %get-tuple-element.158) | copy-start | bytes 3076 | tf_op jit(solution)/shard_map/while
  16.4 3.4 %copy-start.1 = (f32[128,256]{1,0:T(8,128)S(1)}, f32[128,256]{1,0:T(8,128)}, u32[]{:S(2)}) copy-start(f32[128,256]{1,0:T(8,128)} %get-tuple-element.156) | copy-start | bytes 393220 | tf_op jit(solution)/shard_map/while
  16.4 3.4 %copy-start.4 = (f32[256]{0:T(256)S(1)}, f32[256]{0:T(256)}, u32[]{:S(2)}) copy-start(f32[256]{0:T(256)} %get-tuple-element.153) | copy-start | bytes 3076 | tf_op jit(solution)/shard_map/while
  16.4 3.4 %copy-start.5 = (f32[256]{0:T(256)S(1)}, f32[256]{0:T(256)}, u32[]{:S(2)}) copy-start(f32[256]{0:T(256)} %get-tuple-element.157) | copy-start | bytes 3076 | tf_op jit(solution)/shard_map/while
  16.4 3.4 %copy-start.6 = (f32[256]{0:T(256)S(1)}, f32[256]{0:T(256)}, u32[]{:S(2)}) copy-start(f32[256]{0:T(256)} %get-tuple-element.158) | copy-start | bytes 3076 | tf_op jit(solution)/shard_map/while
  23.8 0.6 copy-start.3
  23.8 129.6 %copy-start.7 = (s32[256]{0:T(256)S(1)}, s32[256]{0:T(256)}, u32[]{:S(2)}) copy-start(s32[256]{0:T(256)} %param.17) | copy-start | bytes 3076
  151.8 1.6 copy-start.2
Sparse Core Ops, SparseCore 0:
  24.6 127.1 all-reduce.1
where the time goes:
time: 161 us
  waiting for transfers between devices  127 us (79%)
  between operations  14.1 us (9%)
  other arithmetic  13.6 us (8%)
  local copies, waits for them, and re-layouts  4.04 us (3%)
  matrix products  1.85 us (1%)
    psum x1, waiting for transfers between devices, shards(): lax.psum(lax.map(block_terms, grouped).reshape(event_total, uncertainty.s...  127 us
    reduce_sum x2, other arithmetic, block_terms(): return jnp.sum(losses, axis=2)  7.85 us
    reduce_sum x2, other arithmetic, block_terms(): jnp.sum(jnp.where(hazard_block[:, None, :] == bin_ids, curve_rows[None, :...  4.8 us
  transfers between devices with their start and end apart: 1, of which 1 were waited for; matrix products, arithmetic and copies ran while one was open for 0% of the time, Pallas kernels for 0%

commit v1 on v0

--- a/solution.py
+++ b/solution.py
@@ -47,8 +47,11 @@
 
     block_rows = math.gcd(event_total, target_rows)
     grouped = hazard_bins.reshape(event_total // block_rows, block_rows, hazard_bins.shape[1])
-    summed = lax.psum(
-        lax.map(block_terms, grouped).reshape(event_total, uncertainty.shape[0]), "loc"
+    summed = jnp.sum(
+        lax.all_gather(
+            lax.map(block_terms, grouped).reshape(event_total, uncertainty.shape[0]), "loc"
+        ),
+        axis=0,
     )
     all_events = summed * (1.0 / locations)
     membership = (year_ids[:, None] == year_range[None, :]).astype(jnp.float32)

time: 161 us -> 102 us (0.63)
  waiting for transfers between devices: 127 us -> 64.5 us
  other arithmetic: 13.6 us -> 17 us
    psum x1 -> x0, waiting for transfers between devices: 127 us -> none  [shards(): lax.psum(lax.map(block_terms, grouped).reshape(event_total, uncertainty.s...]
    all_gather x0 -> x1, waiting for transfers between devices: none -> 64.5 us  [shards(): lax.all_gather(lax.map(block_terms, grouped).reshape(event_total, uncerta...]
    reduce_sum x0 -> x1, other arithmetic: none -> 2.4 us  [shards(): jnp.sum(lax.all_gather(lax.map(block_terms, grouped).reshape(event_total,...]
    reduce_sum x2, other arithmetic: 7.85 us -> 9.77 us  [block_terms(): return jnp.sum(losses, axis=2)]
where the time goes in v1:
time: 102 us; the launch traced here: 101 us
  waiting for transfers between devices  64.5 us (63%)
  other arithmetic  17 us (17%)
  between operations  14.1 us (14%)
  local copies, waits for them, and re-layouts  3.88 us (4%)
  matrix products  1.85 us (2%)
    all_gather x1, waiting for transfers between devices, shards(): lax.all_gather(lax.map(block_terms, grouped).reshape(event_total, uncerta...  64.5 us
    reduce_sum x2, other arithmetic, block_terms(): return jnp.sum(losses, axis=2)  9.77 us
    reduce_sum x2, other arithmetic, block_terms(): jnp.sum(jnp.where(hazard_block[:, None, :] == bin_ids, curve_rows[None, :...  4.8 us
    reduce_sum x1, other arithmetic, shards(): jnp.sum(lax.all_gather(lax.map(block_terms, grouped).reshape(event_total,...  2.4 us
  transfers between devices with their start and end apart: 1, of which 1 were waited for; matrix products, arithmetic and copies ran while one was open for 0% of the time, Pallas kernels for 0%

profile of v1, /device:TPU:0, one launch (start us, length us, event | category | flops | bytes accessed | tf_op | source)
XLA Modules:
  0.0 101.4 jit_solution(10905317686049293619)
XLA Ops:
  7.2 0.0 copy-start
  7.2 0.0 all-gather.2.cloned.1.call-start
  7.2 0.8 copy-done
  8.0 0.9 convolution_bitcast_fusion
  8.9 0.0 copy-start.2
  8.9 16.5 %while.11 = (s32[]{:T(128)}, f32[2,128,128]{2,1,0:T(8,128)S(1)}, f32[256]{0:T(256)}, s32[2,128,256]{2,1,0:T(8,128)}, f32[64,256]{1,0:T(8,128)S(1)}, /*index=5*/f...) while((s32[]{:T(128)}, f32[2,128,128]{2,1,0:T(8,128)S(1)}, f32[256]{0:T(256)}, ...), condition=%wide.region_3.4_spmd.clone, body=%wide.region_0.3_spmd.clone.sunk | while | flops 35602432 | bytes 1051757 | solution.py:52
  8.9 0.9 dynamic-slice_bitcast_fusion.2
  9.9 2.4 %select_reduce_fusion.2 = f32[128,256]{1,0:T(8,128)S(1)} fusion(f32[64,256]{1,0:T(8,128)S(1)} %get-tuple-element.155, s32[128,256]{1,0:T(8,128)S(1)} %dynamic-slice_bitcast_fusion.2), kind=kLoop, calls=%fused_computation.3.clone.1 | loop fusion | flops 6258688 | bytes 327680 | tf_op jit(solution)/shard_map/while/body/eval_jaxpr/reduce_sum | solution.py:41
  12.3 4.9 %minimum_reduce_fusion.2 = f32[128,128]{1,0:T(8,128)S(1)} fusion(f32[256]{0:T(256)} %get-tuple-element.158, f32[256]{0:T(256)} %get-tuple-element.157, f32[128,256]{1,0:T(8,128)} %get-tuple-element.156, f32[128,256]{1,0:T(8,128)S(1)} %select_reduce_fusion.2, f32[256]{0:T(256)} %get-tuple-element.153), kind=kLoop, calls=%fused_computation.1.clone.1 | loop fusion | flops 29343744 | bytes 330752 | tf_op jit(solution)/shard_map/while/body/eval_jaxpr/reduce_sum | solution.py:46
  17.2 0.9 dynamic-slice_bitcast_fusion.2
  18.1 2.4 %select_reduce_fusion.2 = f32[128,256]{1,0:T(8,128)S(1)} fusion(f32[64,256]{1,0:T(8,128)S(1)} %get-tuple-element.155, s32[128,256]{1,0:T(8,128)S(1)} %dynamic-slice_bitcast_fusion.2), kind=kLoop, calls=%fused_computation.3.clone.1 | loop fusion | flops 6258688 | bytes 327680 | tf_op jit(solution)/shard_map/while/body/eval_jaxpr/reduce_sum | solution.py:41
  20.5 4.9 %minimum_reduce_fusion.2 = f32[128,128]{1,0:T(8,128)S(1)} fusion(f32[256]{0:T(256)} %get-tuple-element.158, f32[256]{0:T(256)} %get-tuple-element.157, f32[128,256]{1,0:T(8,128)} %get-tuple-element.156, f32[128,256]{1,0:T(8,128)S(1)} %select_reduce_fusion.2, f32[256]{0:T(256)} %get-tuple-element.153), kind=kLoop, calls=%fused_computation.1.clone.1 | loop fusion | flops 29343744 | bytes 330752 | tf_op jit(solution)/shard_map/while/body/eval_jaxpr/reduce_sum | solution.py:46
  25.4 0.0 copy-start.1
  25.4 0.6 copy-done.1
  26.1 0.0 all-gather.2.cloned.1.call-update
  26.1 64.5 %all-gather.2.cloned.1.call-done = f32[32,256,128]{2,1,0:T(8,128)} async-done(((f32[1,256,128]{2,1,0:T(8,128)}), f32[32,256,128]{2,1,0:T(8,128)}) %all-gather.2.cloned.1.call-update) | async-done | bytes 4194320 | tf_op jit(solution)/shard_map/all_gather | solution.py:51
  90.6 2.4 %reduce_sum.27 = f32[256,128]{1,0:T(8,128)S(1)} reduce(f32[32,256,128]{2,1,0:T(8,128)} %all-gather.2.cloned.1.call-done, f32[]{:T(128)} %constant.4.clone.1), dimensions={0}, to_apply=%region_4.5 | reduce | flops 1015808 | bytes 4325380 | tf_op jit(solution)/shard_map/reduce_sum | solution.py:50
  93.0 0.0 copy-done.2
  93.0 1.0 convolution_multiply_fusion
  94.0 0.6 constant_dynamic-slice_fusion
  (4 shorter events, 0.0 us)
Async XLA Ops:
  7.2 0.8 copy-start
  7.2 83.4 %all-gather.2.cloned.1.call-start = ((), (), s32[]{:S(2)}) async-start(), calls=%async_computation | async-start | bytes 4325376 | tf_op jit(solution)/shard_map/all_gather | solution.py:51
  8.9 84.1 %copy-start.2 = (s32[256]{0:T(256)S(1)}, s32[256]{0:T(256)}, u32[]{:S(2)}) copy-start(s32[256]{0:T(256)} %param.17) | copy-start | bytes 3076
  25.4 0.6 copy-start.1
Sparse Core Ops, SparseCore 0:
  26.2 64.3 all-gather.1
